TPU v7x, 32 devices: a whole 2x2x4 slice. The times are simulated.
32 devices in a mesh: rows: 8 (over z, x), cols: 4 (over y, core).
Axes of the slice: x: 2, y: 2, z: 4, core: 2. Of those that a mesh axis runs over, the one named last changes fastest.
Arguments:
- vectors: bfloat16 [1024, 32768], P(None, 'rows'), may hold values from -0.4 to 0.4
- integrals: bfloat16 [2, 256, 32768], P(None, 'cols', 'rows'), may hold values from -8 to 72
- pivots: int32 [2, 256], replicated, may hold values from 0 to 32767, as said below
Outputs:
- new_vectors: float32 [2, 256, 32768], P(None, 'cols', 'rows')
Inputs may be any that keep to these rules, and one draw needn't show every extreme that they name: The 2 x 256 entries are distinct shell-pair rows. In each panel the rows of one index of rows (an aligned block of 4096) hold at most 64 pivots, and some block holds exactly 64.
All inputs are finite; a program needn't handle non-finite values.
Results may differ from a plain program's by a relative error of at most 0.00036.
Values may be sent and summed in bfloat16 or wider, within the bound.
No kernel may reach another device: no remote copies, remote signals or barrier semaphores. Data moves between devices by JAX's collectives and lax.ppermute only.
A program may use at most 64 MiB of HBM per device.

v0:
```python
import jax
import jax.numpy as jnp
from jax import lax
from jax.sharding import PartitionSpec as P

PW = 256
PANELS = 2


def select_matrix(row_count, targets):
    return (jnp.arange(row_count, dtype=jnp.int32)[:, None] == targets[None, :]).astype(
        jnp.bfloat16
    )


def transposed_product(left, right):
    return lax.dot_general(
        left, right, (((0,), (0,)), ((), ())), preferred_element_type=jnp.float32
    )


def solve_block(lower_factor, residual):
    return jax.scipy.linalg.solve_triangular(lower_factor, residual, lower=True)


def per_device(vectors, integrals, pivots):
    row_count = vectors.shape[1]
    block_cols = integrals.shape[1]
    owners = lax.axis_size("rows")
    owner_index = lax.axis_index("rows")
    owner_start = owner_index * row_count
    col_start = lax.axis_index("cols") * block_cols
    factors = [vectors]
    results = []
    for panel in range(PANELS):
        pivot_row = pivots[panel]
        local_targets = pivot_row - owner_start
        slot_count = 2 * PW // owners
        owner_of = pivot_row // row_count
        order = jnp.arange(PW, dtype=jnp.int32)
        earlier = (owner_of[None, :] == owner_of[:, None]) & (order[None, :] < order[:, None])
        slot_rank = jnp.sum(earlier.astype(jnp.int32), axis=1)
        mine = owner_of == owner_index
        slot_pick = (
            (slot_rank[:, None] == jnp.arange(slot_count, dtype=jnp.int32)[None, :]) & mine[:, None]
        ).astype(jnp.bfloat16)
        slot_select = jnp.dot(
            select_matrix(row_count, local_targets), slot_pick, preferred_element_type=jnp.float32
        ).astype(jnp.bfloat16)
        sending = jnp.concatenate(
            [
                jnp.dot(factor, slot_select, preferred_element_type=jnp.float32)
                for factor in factors
            ],
            axis=0,
        ).astype(jnp.bfloat16)
        targets = lax.dynamic_slice_in_dim(owner_of * slot_count + slot_rank, col_start, block_cols)
        receive_pick = select_matrix(owners * slot_count, targets)
        picked = jnp.dot(
            lax.all_gather(sending, "rows", axis=1, tiled=True),
            receive_pick,
            preferred_element_type=jnp.float32,
        ).astype(jnp.bfloat16)
        residual = integrals[panel].astype(jnp.float32)
        offset = 0
        for factor in factors:
            residual = residual - transposed_product(
                picked[offset : offset + factor.shape[0]], factor
            )
            offset = offset + factor.shape[0]
        every_pivot = select_matrix(row_count, local_targets).astype(jnp.float32)
        contribution = jnp.dot(residual, every_pivot, precision=lax.Precision.HIGHEST)
        placed = lax.dynamic_update_slice(
            jnp.zeros((PW, PW), jnp.float32), contribution, (col_start, 0)
        )
        block = lax.psum(placed, ("rows", "cols"))
        lower_factor = jnp.linalg.cholesky(0.5 * (block + block.T))
        whole = lax.all_gather(residual, "cols", axis=0, tiled=True)
        solved = solve_block(lower_factor, whole)
        fresh = lax.dynamic_slice_in_dim(solved, col_start, block_cols, 0)
        if panel + 1 < PANELS:
            factors.append(solved.astype(jnp.bfloat16))
        results.append(fresh)
    return jnp.stack(results)


def solution(mesh):
    placed = (P(None, "rows"), P(None, "cols", "rows"), P())
    return jax.shard_map(
        per_device, mesh=mesh, in_specs=placed, out_specs=P(None, "cols", "rows"), check_vma=False
    )
```

profile of v0, /device:TPU:0, one launch (start us, length us, event | category | flops | bytes accessed | tf_op | source)
XLA Modules:
  0.0 519.9 jit_solution(4560592978291593466)
XLA Ops:
  7.5 7.5 %fusion.14 = bf16[1024,64]{0,1:T(8,128)(2,1)} fusion(bf16[1024,4096]{1,0:T(8,128)(2,1)} %param.6, s32[256]{0:T(256)S(1)} %bitcast.98, s32[256]{0:T(256)S(1)} %convert_reduce_fusion.1, pred[256]{0:T(512)(128)(4,1)S(1)} %get-tuple-element.65), kind=kOutput, calls=%fused_computation.36 | convolution fusion | flops 672497664 | bytes 8521984 | tf_op jit(solution)/shard_map/dot_general | solution.py:52
  15.2 43.0 %all-gather.5.cloned.1.call-done = bf16[1024,512]{0,1:T(8,128)(2,1)} async-done(((bf16[1024,64]{0,1:T(8,128)(2,1)}), bf16[1024,512]{0,1:T(8,128)(2,1)}) %all-gather.5.cloned.1.call-update) | async-done | bytes 1048592 | tf_op jit(solution)/shard_map/all_gather | solution.py:60
  58.2 5.9 %convolution_subtract_fusion.4 = f32[64,4096]{1,0:T(8,128)S(1)} fusion(bf16[1024,4096]{1,0:T(8,128)(2,1)} %param.6, bf16[1024,512]{0,1:T(8,128)(2,1)} %all-gather.5.cloned.1.call-done, bf16[2,64,4096]{2,1,0:T(8,128)(2,1)S(1)} %copy-done.6, s32[64]{0:T(128)S(1)} %dynamic_slice.12), kind=kOutput, calls=%fused_computation.12 | convolution fusion | flops 604602368 | bytes 11010304 | tf_op jit(solution)/shard_map/dot_general | solution.py:17
  68.7 6.1 %fusion.13 = bf16[1024,64]{0,1:T(8,128)(2,1)S(1)} fusion(bf16[4096,64]{0,1:T(8,128)(2,1)S(1)} %convolution_convert_fusion.1, bf16[1024,4096]{1,0:T(8,128)(2,1)} %param.6), kind=kOutput, calls=%fused_computation.35 | convolution fusion | flops 536936448 | bytes 9043968 | tf_op jit(solution)/shard_map/dot_general | solution.py:52
  74.7 117.2 %all-reduce.4.cloned.1.call-done = f32[256,256]{1,0:T(8,128)} async-done(((f32[256,256]{1,0:T(8,128)}), f32[256,256]{1,0:T(8,128)}) %all-reduce.4.cloned.1.call-update) | async-done | bytes 262160 | tf_op jit(solution)/shard_map/psum | solution.py:76
  194.2 11.7 %cholesky.130 = f32[128,128]{1,0:T(8,128)S(1)} custom-call(f32[128,128]{1,0:T(8,128)S(1)} %cholesky.194), custom_call_target="Cholesky" | custom-call | tf_op jit(solution)/shard_map/jit(cholesky)/cholesky | solution.py:77
  206.0 9.8 %custom-call.13 = f32[1,128,128]{1,2,0:T(8,128)S(1)} custom-call(f32[1,128,128]{2,1,0:T(8,128)S(1)} %get-tuple-element.54), custom_call_target="InvertDiagBlocksLowerTriangular" | custom-call | tf_op jit(solution)/shard_map/jit(cholesky)/cholesky | solution.py:77
  216.3 11.9 %cholesky.147 = f32[128,128]{1,0:T(8,128)S(1)} custom-call(f32[128,128]{1,0:T(8,128)S(1)} %convolution_subtract_fusion.6), custom_call_target="Cholesky" | custom-call | tf_op jit(solution)/shard_map/jit(cholesky)/cholesky | solution.py:77
  231.0 4.1 while.4
  235.1 19.7 %custom-call.14 = f32[2,128,128]{1,2,0:T(8,128)S(1)} custom-call(f32[2,128,128]{2,1,0:T(8,128)S(1)} %get-tuple-element.21), custom_call_target="InvertDiagBlocksLowerTriangular" | custom-call | tf_op jit(solution)/shard_map/jit(_solve_triangular)/triangular_solve | solution.py:23
  254.8 3.6 fusion.5
  258.5 1.9 convolution_subtract_fusion.1
  260.4 1.9 fusion.42
  264.6 40.9 %all-gather.9.cloned.1.call-done = bf16[1280,512]{0,1:T(8,128)(2,1)} async-done(((bf16[1280,64]{0,1:T(8,128)(2,1)}), bf16[1280,512]{0,1:T(8,128)(2,1)}) %all-gather.9.cloned.1.call-update) | async-done | bytes 1310736 | tf_op jit(solution)/shard_map/all_gather | solution.py:60
  307.2 5.1 convolution_subtract_fusion.3
  316.0 124.8 %all-reduce.6.cloned.1.call-done = f32[256,256]{1,0:T(8,128)} async-done(((f32[256,256]{1,0:T(8,128)}), f32[256,256]{1,0:T(8,128)}) %all-reduce.6.cloned.1.call-update) | async-done | bytes 262160 | tf_op jit(solution)/shard_map/psum | solution.py:76
  443.3 11.7 %cholesky.164 = f32[128,128]{1,0:T(8,128)S(1)} custom-call(f32[128,128]{1,0:T(8,128)S(1)} %cholesky.197), custom_call_target="Cholesky" | custom-call | tf_op jit(solution)/shard_map/jit(cholesky)/cholesky | solution.py:77
  455.0 9.8 %custom-call.15 = f32[1,128,128]{1,2,0:T(8,128)S(1)} custom-call(f32[1,128,128]{2,1,0:T(8,128)S(1)} %get-tuple-element.50), custom_call_target="InvertDiagBlocksLowerTriangular" | custom-call | tf_op jit(solution)/shard_map/jit(cholesky)/cholesky | solution.py:77
  465.4 11.7 %cholesky.181 = f32[128,128]{1,0:T(8,128)S(1)} custom-call(f32[128,128]{1,0:T(8,128)S(1)} %convolution_subtract_fusion.5), custom_call_target="Cholesky" | custom-call | tf_op jit(solution)/shard_map/jit(cholesky)/cholesky | solution.py:77
  479.7 4.1 while.5
  483.9 19.7 %custom-call.16 = f32[2,128,128]{1,2,0:T(8,128)S(1)} custom-call(f32[2,128,128]{2,1,0:T(8,128)S(1)} %get-tuple-element.22), custom_call_target="InvertDiagBlocksLowerTriangular" | custom-call | tf_op jit(solution)/shard_map/jit(_solve_triangular)/triangular_solve | solution.py:23
  503.6 3.6 fusion.3
  507.2 1.9 convolution_subtract_fusion
  509.2 1.9 fusion.38
  (98 shorter events, 31.4 us)
Async XLA Ops:
  6.5 51.7 %all-gather.5.cloned.1.call-start = ((), (), s32[]{:S(2)}) async-start(), calls=%async_computation | async-start | bytes 1179648 | tf_op jit(solution)/shard_map/all_gather | solution.py:60
  7.5 50.7 %copy-start.6 = (bf16[2,64,4096]{2,1,0:T(8,128)(2,1)S(1)}, bf16[2,64,4096]{2,1,0:T(8,128)(2,1)}, u32[]{:S(2)}) copy-start(bf16[2,64,4096]{2,1,0:T(8,128)(2,1)} %param.7) | copy-start | bytes 3145732
  15.0 176.9 %all-reduce.4.cloned.1.call-start = ((), (), s32[]{:S(2)}) async-start(), calls=%async_computation.1 | async-start | bytes 524288 | tf_op jit(solution)/shard_map/psum | solution.py:76
  64.1 2.5 copy-start.5
  65.8 0.7 copy-start.8
  66.5 188.3 %all-gather.7.cloned.1.call-start = ((), (), s32[]{:S(2)}) async-start(), calls=%async_computation.2 | async-start | bytes 5242880 | tf_op jit(solution)/shard_map/all_gather | solution.py:78
  67.3 238.2 %all-gather.9.cloned.1.call-start = ((), (), s32[]{:S(2)}) async-start(), calls=%async_computation.3 | async-start | bytes 1474560 | tf_op jit(solution)/shard_map/all_gather | solution.py:60
  254.8 3.7 copy-start.2
  262.4 1.3 copy-start
  263.7 43.5 %copy-start.7 = (bf16[2,64,4096]{2,1,0:T(8,128)(2,1)S(1)}, bf16[2,64,4096]{2,1,0:T(8,128)(2,1)}, u32[]{:S(2)}) copy-start(bf16[2,64,4096]{2,1,0:T(8,128)(2,1)} %param.7) | copy-start | bytes 3145732
  264.4 176.4 %all-reduce.6.cloned.1.call-start = ((), (), s32[]{:S(2)}) async-start(), calls=%async_computation.4 | async-start | bytes 524288 | tf_op jit(solution)/shard_map/psum | solution.py:76
  307.2 5.2 copy-start.1
  312.9 2.9 copy-start.4
  314.6 0.7 copy-start.9
  315.3 188.3 %all-gather.11.cloned.1.call-start = ((), (), s32[]{:S(2)}) async-start(), calls=%async_computation.5 | async-start | bytes 5242880 | tf_op jit(solution)/shard_map/all_gather | solution.py:78
  503.6 3.7 copy-start.3
Sparse Core Ops, SparseCore 0:
  15.2 42.9 all-gather.4
  66.6 125.2 all-reduce.3
  193.5 33.7 all-gather.6
  264.5 40.8 all-gather.8
  315.4 125.3 all-reduce.5
  442.3 33.6 all-gather.10
where the time goes:
time: 525 us; the launch traced here: 520 us
  waiting for transfers between devices  327 us (62%)
  other arithmetic  115 us (22%)
  matrix products  47.8 us (9%)
  between operations  16.7 us (3%)
  local copies, waits for them, and re-layouts  12.8 us (2%)
    psum x2, waiting for transfers between devices, per_device(): block = lax.psum(placed, ('rows', 'cols'))  242 us
    all_gather x2, waiting for transfers between devices, per_device(): lax.all_gather(sending, 'rows', axis=1, tiled=True)  83.9 us
    another operation x14, other arithmetic, per_device(): lower_factor = jnp.linalg.cholesky(0.5 * (block + block.T))  69.4 us
    another operation x5, other arithmetic, solve_block(): return jax.scipy.linalg.solve_triangular(lower_factor, residual, lower=True)  39.4 us
    another operation x6, matrix products, solve_block(): return jax.scipy.linalg.solve_triangular(lower_factor, residual, lower=True)  15 us
    dot_general x3, matrix products, per_device(): jnp.dot(factor, slot_select, preferred_element_type=jnp.float32)  14.4 us
    dot_general x3, matrix products, transposed_product(): lax.dot_general(left, right, (((0,), (0,)), ((), ())), preferred_element_...  11.5 us
  transfers between devices with their start and end apart: 6, of which 4 were waited for; matrix products, arithmetic and copies ran while one was open for 25% of the time, Pallas kernels for 0%

commit v1 on v0

--- a/solution.py
+++ b/solution.py
@@ -73,7 +73,7 @@
         placed = lax.dynamic_update_slice(
             jnp.zeros((PW, PW), jnp.float32), contribution, (col_start, 0)
         )
-        block = lax.psum(placed, ("rows", "cols"))
+        block = jnp.sum(lax.all_gather(placed, axis_name=("rows", "cols")), axis=0)
         lower_factor = jnp.linalg.cholesky(0.5 * (block + block.T))
         whole = lax.all_gather(residual, "cols", axis=0, tiled=True)
         solved = solve_block(lower_factor, whole)

time: 525 us -> 429 us (0.82)
  waiting for transfers between devices: 327 us -> 228 us
  other arithmetic: 115 us -> 121 us
    psum x2 -> x0, waiting for transfers between devices: 242 us -> none  [per_device(): block = lax.psum(placed, ('rows', 'cols'))]
    all_gather x0 -> x2, waiting for transfers between devices: none -> 143 us  [per_device(): block = jnp.sum(lax.all_gather(placed, axis_name=('rows', 'cols')), axis=0)]
    reduce_sum x0 -> x2, other arithmetic: none -> 7.86 us  [per_device(): block = jnp.sum(lax.all_gather(placed, axis_name=('rows', 'cols')), axis=0)]
  transfers between devices with their start and end apart: 6 -> 6, of which waited for: 4 -> 4; matrix products, arithmetic and copies ran while one was open for 25% -> 32% of each run, Pallas kernels for 0% -> 0%
where the time goes in v1:
time: 429 us; the launch traced here: 424 us
  waiting for transfers between devices  228 us (53%)
  other arithmetic  121 us (28%)
  matrix products  47.6 us (11%)
  between operations  16.7 us (4%)
  local copies, waits for them, and re-layouts  10.5 us (2%)
    all_gather x2, waiting for transfers between devices, per_device(): block = jnp.sum(lax.all_gather(placed, axis_name=('rows', 'cols')), axis=0)  143 us
    all_gather x2, waiting for transfers between devices, per_device(): lax.all_gather(sending, 'rows', axis=1, tiled=True)  83.5 us
    another operation x14, other arithmetic, per_device(): lower_factor = jnp.linalg.cholesky(0.5 * (block + block.T))  69.6 us
    another operation x5, other arithmetic, solve_block(): return jax.scipy.linalg.solve_triangular(lower_factor, residual, lower=True)  39.4 us
    another operation x6, matrix products, solve_block(): return jax.scipy.linalg.solve_triangular(lower_factor, residual, lower=True)  15 us
    dot_general x3, matrix products, per_device(): jnp.dot(factor, slot_select, preferred_element_type=jnp.float32)  14.5 us
    dot_general x3, matrix products, transposed_product(): lax.dot_general(left, right, (((0,), (0,)), ((), ())), preferred_element_...  11.2 us
  transfers between devices with their start and end apart: 6, of which 4 were waited for; matrix products, arithmetic and copies ran while one was open for 32% of the time, Pallas kernels for 0%

profile of v1, /device:TPU:0, one launch (start us, length us, event | category | flops | bytes accessed | tf_op | source)
XLA Modules:
  0.0 424.1 jit_solution(181477910736636313)
XLA Ops:
  7.5 7.6 %fusion.14 = bf16[1024,64]{0,1:T(8,128)(2,1)} fusion(bf16[1024,4096]{1,0:T(8,128)(2,1)} %param.6, s32[256]{0:T(256)S(1)} %bitcast.108, s32[256]{0:T(256)S(1)} %convert_reduce_fusion.1, pred[256]{0:T(512)(128)(4,1)S(1)} %get-tuple-element.65), kind=kOutput, calls=%fused_computation.36 | convolution fusion | flops 672497664 | bytes 8521984 | tf_op jit(solution)/shard_map/dot_general | solution.py:52
  15.3 43.0 %all-gather.7.cloned.1.call-done = bf16[1024,512]{0,1:T(8,128)(2,1)} async-done(((bf16[1024,64]{0,1:T(8,128)(2,1)}), bf16[1024,512]{0,1:T(8,128)(2,1)}) %all-gather.7.cloned.1.call-update) | async-done | bytes 1048592 | tf_op jit(solution)/shard_map/all_gather | solution.py:60
  58.4 5.6 %convolution_subtract_fusion.4 = f32[64,4096]{1,0:T(8,128)S(1)} fusion(bf16[1024,4096]{1,0:T(8,128)(2,1)} %param.6, bf16[1024,512]{0,1:T(8,128)(2,1)} %all-gather.7.cloned.1.call-done, bf16[2,64,4096]{2,1,0:T(8,128)(2,1)S(1)} %copy-done.6, s32[64]{0:T(128)S(1)} %dynamic_slice.12), kind=kOutput, calls=%fused_computation.11 | convolution fusion | flops 604602368 | bytes 11010304 | tf_op jit(solution)/shard_map/dot_general | solution.py:17
  68.5 6.0 %fusion.13 = bf16[1024,64]{0,1:T(8,128)(2,1)S(1)} fusion(bf16[4096,64]{0,1:T(8,128)(2,1)S(1)} %convolution_convert_fusion, bf16[1024,4096]{1,0:T(8,128)(2,1)} %param.6), kind=kOutput, calls=%fused_computation.35 | convolution fusion | flops 536936448 | bytes 9043968 | tf_op jit(solution)/shard_map/dot_general | solution.py:52
  74.5 67.8 %all-gather.9.cloned.1.call-done = f32[32,256,256]{2,1,0:T(8,128)} async-done(((f32[1,256,256]{2,1,0:T(8,128)}), f32[32,256,256]{2,1,0:T(8,128)}) %all-gather.9.cloned.1.call-update) | async-done | bytes 8388624 | tf_op jit(solution)/shard_map/all_gather | solution.py:76
  142.3 3.9 reduce_sum.37
  146.6 11.7 %cholesky.130 = f32[128,128]{1,0:T(8,128)S(1)} custom-call(f32[128,128]{1,0:T(8,128)S(1)} %cholesky.194), custom_call_target="Cholesky" | custom-call | tf_op jit(solution)/shard_map/jit(cholesky)/cholesky | solution.py:77
  158.3 9.8 %custom-call.13 = f32[1,128,128]{1,2,0:T(8,128)S(1)} custom-call(f32[1,128,128]{2,1,0:T(8,128)S(1)} %get-tuple-element.54), custom_call_target="InvertDiagBlocksLowerTriangular" | custom-call | tf_op jit(solution)/shard_map/jit(cholesky)/cholesky | solution.py:77
  168.7 12.1 %cholesky.147 = f32[128,128]{1,0:T(8,128)S(1)} custom-call(f32[128,128]{1,0:T(8,128)S(1)} %convolution_subtract_fusion.6), custom_call_target="Cholesky" | custom-call | tf_op jit(solution)/shard_map/jit(cholesky)/cholesky | solution.py:77
  183.4 3.8 while.4
  187.2 19.7 %custom-call.14 = f32[2,128,128]{1,2,0:T(8,128)S(1)} custom-call(f32[2,128,128]{2,1,0:T(8,128)S(1)} %get-tuple-element.21), custom_call_target="InvertDiagBlocksLowerTriangular" | custom-call | tf_op jit(solution)/shard_map/jit(_solve_triangular)/triangular_solve | solution.py:23
  206.9 3.6 fusion.5
  212.5 1.9 fusion.45
  216.6 40.5 %all-gather.13.cloned.1.call-done = bf16[1280,512]{0,1:T(8,128)(2,1)} async-done(((bf16[1280,64]{0,1:T(8,128)(2,1)}), bf16[1280,512]{0,1:T(8,128)(2,1)}) %all-gather.13.cloned.1.call-update) | async-done | bytes 1310736 | tf_op jit(solution)/shard_map/all_gather | solution.py:60
  258.8 5.1 %convolution_subtract_fusion.3 = f32[64,4096]{1,0:T(8,128)S(1)} fusion(bf16[1024,4096]{1,0:T(8,128)(2,1)} %param.6, bf16[2,64,4096]{2,1,0:T(8,128)(2,1)S(1)} %copy-done.7, bf16[1280,64]{0,1:T(8,128)(2,1)S(1)} %convolution_convert_fusion.2), kind=kOutput, calls=%fused_computation.10 | convolution fusion | flops 537395200 | bytes 10092544 | tf_op jit(solution)/shard_map/dot_general | solution.py:17
  267.6 75.3 %all-gather.15.cloned.1.call-done = f32[32,256,256]{2,1,0:T(8,128)} async-done(((f32[1,256,256]{2,1,0:T(8,128)}), f32[32,256,256]{2,1,0:T(8,128)}) %all-gather.15.cloned.1.call-update) | async-done | bytes 8388624 | tf_op jit(solution)/shard_map/all_gather | solution.py:76
  342.9 3.9 reduce_sum.39
  347.2 11.7 %cholesky.164 = f32[128,128]{1,0:T(8,128)S(1)} custom-call(f32[128,128]{1,0:T(8,128)S(1)} %cholesky.197), custom_call_target="Cholesky" | custom-call | tf_op jit(solution)/shard_map/jit(cholesky)/cholesky | solution.py:77
  359.0 9.8 %custom-call.15 = f32[1,128,128]{1,2,0:T(8,128)S(1)} custom-call(f32[1,128,128]{2,1,0:T(8,128)S(1)} %get-tuple-element.50), custom_call_target="InvertDiagBlocksLowerTriangular" | custom-call | tf_op jit(solution)/shard_map/jit(cholesky)/cholesky | solution.py:77
  369.3 11.7 %cholesky.181 = f32[128,128]{1,0:T(8,128)S(1)} custom-call(f32[128,128]{1,0:T(8,128)S(1)} %convolution_subtract_fusion.5), custom_call_target="Cholesky" | custom-call | tf_op jit(solution)/shard_map/jit(cholesky)/cholesky | solution.py:77
  383.8 4.3 %while.5 = (s32[]{:T(128)}, f32[256,256]{1,0:T(8,128)S(1)}, s32[2,2]{1,0:T(2,128)S(1)}, f32[2,128,128]{2,1,0:T(8,128)S(1)}, s32[]{:T(128)}) while((s32[]{:T(128)}, f32[256,256]{1,0:T(8,128)S(1)}, s32[2,2]{1,0:T(2,128)S(1)}, f32[2,128,128]{2,1,0:T(8,128)S(1)}, s32[]{:T(128)}) %tuple.69), condition=%wide.while_cond.clone, body=%wide.while_body.clone.sunk | while | flops 2 | bytes 131189 | solution.py:23
  388.1 19.7 %custom-call.16 = f32[2,128,128]{1,2,0:T(8,128)S(1)} custom-call(f32[2,128,128]{2,1,0:T(8,128)S(1)} %get-tuple-element.22), custom_call_target="InvertDiagBlocksLowerTriangular" | custom-call | tf_op jit(solution)/shard_map/jit(_solve_triangular)/triangular_solve | solution.py:23
  407.8 3.6 fusion.3
  413.4 1.9 fusion.41
  (98 shorter events, 31.0 us)
Async XLA Ops:
  6.5 51.8 %all-gather.7.cloned.1.call-start = ((), (), s32[]{:S(2)}) async-start(), calls=%async_computation | async-start | bytes 1179648 | tf_op jit(solution)/shard_map/all_gather | solution.py:60
  7.5 50.8 %copy-start.6 = (bf16[2,64,4096]{2,1,0:T(8,128)(2,1)S(1)}, bf16[2,64,4096]{2,1,0:T(8,128)(2,1)}, u32[]{:S(2)}) copy-start(bf16[2,64,4096]{2,1,0:T(8,128)(2,1)} %param.7) | copy-start | bytes 3145732
  15.2 127.1 %all-gather.9.cloned.1.call-start = ((), (), s32[]{:S(2)}) async-start(), calls=%async_computation.1 | async-start | bytes 8650752 | tf_op jit(solution)/shard_map/all_gather | solution.py:76
  63.9 2.5 copy-start.5
  65.6 0.7 copy-start.8
  66.4 140.5 %all-gather.11.cloned.1.call-start = ((), (), s32[]{:S(2)}) async-start(), calls=%async_computation.2 | async-start | bytes 5242880 | tf_op jit(solution)/shard_map/all_gather | solution.py:78
  67.1 190.0 %all-gather.13.cloned.1.call-start = ((), (), s32[]{:S(2)}) async-start(), calls=%async_computation.3 | async-start | bytes 1474560 | tf_op jit(solution)/shard_map/all_gather | solution.py:60
  206.9 3.7 copy-start.2
  214.4 1.3 copy-start
  215.7 43.0 %copy-start.7 = (bf16[2,64,4096]{2,1,0:T(8,128)(2,1)S(1)}, bf16[2,64,4096]{2,1,0:T(8,128)(2,1)}, u32[]{:S(2)}) copy-start(bf16[2,64,4096]{2,1,0:T(8,128)(2,1)} %param.7) | copy-start | bytes 3145732
  216.5 126.5 %all-gather.15.cloned.1.call-start = ((), (), s32[]{:S(2)}) async-start(), calls=%async_computation.4 | async-start | bytes 8650752 | tf_op jit(solution)/shard_map/all_gather | solution.py:76
  258.8 5.2 %copy-start.1 = (f32[128,4096]{1,0:T(8,128)S(1)}, f32[128,4096]{1,0:T(8,128)}, u32[]{:S(2)}) copy-start(f32[128,4096]{1,0:T(8,128)} %copy-done) | copy-start | bytes 6291460
  264.4 2.7 copy-start.4
  266.2 0.7 copy-start.9
  266.9 140.9 %all-gather.17.cloned.1.call-start = ((), (), s32[]{:S(2)}) async-start(), calls=%async_computation.5 | async-start | bytes 5242880 | tf_op jit(solution)/shard_map/all_gather | solution.py:78
  407.8 3.7 copy-start.3
Sparse Core Ops, SparseCore 0:
  15.3 42.9 all-gather.6
  66.5 75.7 all-gather.8
  143.9 33.1 all-gather.10
  216.6 40.4 all-gather.12
  267.0 75.8 all-gather.14
  344.3 33.2 all-gather.16
